TPU v7x, 32 devices: a whole 2x2x4 slice. The times are simulated.
32 devices in a mesh: gz: 4 (over x, core), xy: 8 (over z, y).
Axes of the slice: x: 2, y: 2, z: 4, core: 2. Of those that a mesh axis runs over, the one named last changes fastest.
Arguments:
- thermal_load: float32 [64, 4, 128, 384], P('gz', None, 'xy'), may hold values from -12 to 12
- material: int32 [64, 128, 384], P('gz', 'xy'), may hold values from 0 to 7
- layer_ids: int32 [64, 128, 384], P('gz', 'xy'), may hold values from 0 to 5
- stiffness: float32 [8, 4, 4], replicated, may hold values from -0.7 to 13, as said below
- coupling: float32 [6, 4, 4], replicated, may hold values from -0.15 to 0.9, as said below
- pivots: float32 [8, 4, 4], replicated, may hold values from -0.015 to 0.14, as said below
- factor: float32 [6, 4, 4], replicated, may hold values from -0.01 to 1
Outputs:
- solution: float32 [64, 4, 128, 384], P('gz', None, 'xy')
- residual: float32 [64, 4, 128, 384], P('gz', None, 'xy')
Inputs may be any that keep to these rules, and one draw needn't show every extreme that they name: `stiffness`: each block is symmetric, and the operator A of the steps is positive definite. `coupling`: each block is symmetric. `pivots`: each block is symmetric positive definite.
All inputs are finite; a program needn't handle non-finite values.
Results may differ from a plain program's by a relative error of at most 0.0003.
Values sent between devices are 32-bit elements; how exact they have to be, the bound alone decides.
A program may use at most 192 MiB of HBM per device.

v0:
```python
import functools

import jax
import jax.numpy as jnp
from jax import lax
from jax.experimental import pallas as pl
from jax.experimental.pallas import tpu as pltpu
from jax.sharding import PartitionSpec as P

MESH = pl.DeviceIdType.MESH
PAIRS = [(i, j) for i in range(4) for j in range(i, 4)]
SYM = {}
for _k, (_i, _j) in enumerate(PAIRS):
    SYM[_i, _j] = _k
    SYM[_j, _i] = _k
UP, DOWN, PUSH, PLANE, LOW, HIGH = range(6)


def pick(values, bits):
    level = 0
    while len(values) > 1:
        merged = []
        for i in range(0, len(values) - 1, 2):
            merged.append(jnp.where(bits[level], values[i + 1], values[i]))
        if len(values) % 2:
            merged.append(values[-1])
        values = merged
        level += 1
    return values[0]


def bit_masks(labels, entries):
    count = max(1, (entries - 1).bit_length())
    return [(labels & (1 << b)) != 0 for b in range(count)]


def total(terms):
    return (terms[0] + terms[1]) + (terms[2] + terms[3])


def kernel(
    n, m,
    load_ref, mat_ref, lay_ref, stiff_ref, coup_ref, piv_ref, fact_ref,
    sol_ref, res_ref,
    kc, cc, sc, pc, tc, u, au,
    up_send, up_recv, dn_send, dn_recv, push_send, push_recv, plane_recv,
    halo_send, halo_recv, gbuf, xbuf,
    send_sem, recv_sem, gs_sem, gr_sem, xs_sem, xr_sem,
):
    depth, _, nx, ny = load_ref.shape
    me = lax.axis_index("gz")
    side = lax.axis_index("xy")
    not_first, not_last = me > 0, me < n - 1
    has_left, has_right = side > 0, side < m - 1

    barrier = pltpu.get_barrier_semaphore()
    for k in range(1, n):
        pl.semaphore_signal(
            barrier, inc=1, device_id={"gz": lax.rem(me + k, n)}, device_id_type=MESH
        )
    for k in range(1, m):
        pl.semaphore_signal(
            barrier, inc=1, device_id={"xy": lax.rem(side + k, m)}, device_id_type=MESH
        )

    def neighbour(axis, step):
        if axis == "gz":
            return {"gz": lax.rem(me + step + n, n)}
        return {"xy": lax.rem(side + step + m, m)}

    def remote(src, dst, it, kind, axis, step):
        return pltpu.make_async_remote_copy(
            src_ref=src, dst_ref=dst, send_sem=send_sem.at[it, kind],
            recv_sem=recv_sem.at[it, kind], device_id=neighbour(axis, step),
            device_id_type=MESH,
        )

    def copy(it, kind):
        if kind == UP:
            return remote(up_send.at[it], up_recv.at[it], it, UP, "gz", 1)
        if kind == DOWN:
            return remote(dn_send.at[it], dn_recv.at[it], it, DOWN, "gz", -1)
        if kind == PUSH:
            return remote(push_send.at[it], push_recv.at[it], it, PUSH, "gz", 1)
        if kind == PLANE:
            return remote(u.at[it, 1], plane_recv.at[it], it, PLANE, "gz", -1)
        if kind == LOW:
            return remote(halo_send.at[it, 0], halo_recv.at[it, 1], it, LOW, "xy", -1)
        return remote(halo_send.at[it, 1], halo_recv.at[it, 0], it, HIGH, "xy", 1)

    senders = {UP: not_last, DOWN: not_first, PUSH: not_last, PLANE: not_first,
               LOW: has_left, HIGH: has_right}
    receivers = {UP: not_first, DOWN: not_last, PUSH: not_first, PLANE: not_last,
                 LOW: has_right, HIGH: has_left}

    def start(it, kind):
        @pl.when(senders[kind])
        def _():
            copy(it, kind).start()

    def arrive(it, kind):
        @pl.when(receivers[kind])
        def _():
            copy(it, kind).wait_recv()

    zero_plane = jnp.zeros((4, nx, ny), jnp.float32)

    @pl.when(me == 0)
    def _():
        for it in range(2):
            up_recv[it] = zero_plane
            push_recv[it] = zero_plane

    @pl.when(me == n - 1)
    def _():
        for it in range(2):
            dn_recv[it] = zero_plane
            plane_recv[it] = zero_plane

    @pl.when(side == 0)
    def _():
        for it in range(2):
            halo_recv[it, 0] = jnp.zeros((depth, 4, ny), jnp.float32)

    @pl.when(side == m - 1)
    def _():
        for it in range(2):
            halo_recv[it, 1] = jnp.zeros((depth, 4, ny), jnp.float32)

    for it in range(2):
        u[it, 0] = zero_plane
        u[it, depth + 1] = zero_plane
    for k in range(10):
        cc[0, k] = jnp.zeros((nx, ny), jnp.float32)

    def fill(table, label_ref, out, entries_of, offset):
        entries = table.shape[0]

        def plane(z, carry):
            for t in range(0, ny, 128):
                bits = bit_masks(label_ref[z, :, t:t + 128], entries)
                for k, (i, j) in enumerate(entries_of):
                    values = [
                        jnp.full((nx, 128), table[e, i, j], jnp.float32) for e in range(entries)
                    ]
                    out[z + offset, k, :, t:t + 128] = pick(values, bits)
            return carry

        lax.fori_loop(0, depth, plane, 0)

    def fill_rest():
        fill(piv_ref, mat_ref, sc, PAIRS, 0)
        fill(stiff_ref, mat_ref, kc, PAIRS, 0)
        fill(coup_ref, lay_ref, cc, PAIRS, 1)

    fill(fact_ref, lay_ref, pc, [(i, j) for i in range(4) for j in range(4)], 0)

    def sym_apply(ref, z, v):
        return [total([ref[z, SYM[i, j]] * v[j] for j in range(4)]) for i in range(4)]

    def lift(z, v):
        return [total([pc[z, 4 * i + j] * v[j] for j in range(4)]) for i in range(4)]

    def drop(z, v):
        return [total([pc[z, 4 * j + i] * v[j] for j in range(4)]) for i in range(4)]

    def zeros4():
        return tuple(jnp.zeros((nx, ny), jnp.float32) for _ in range(4))

    def climb(src, it, z, carried, keep):
        moved = lift(z, carried)
        carried = [src[z, c] + moved[c] for c in range(4)]
        if keep:
            scaled = sym_apply(sc, z, carried)
            for c in range(4):
                u[it, z + 1, c] = scaled[c]
        return tuple(carried)

    def build_transfer():
        for x in range(0, nx, 8):
            for t in range(0, ny, 128):
                def level(z, now):
                    p = [pc[z, k, x:x + 8, t:t + 128] for k in range(16)]
                    return tuple(
                        total([p[4 * i + k] * now[4 * k + j] for k in range(4)])
                        for i in range(4) for j in range(4)
                    )

                now = tuple(pc[0, k, x:x + 8, t:t + 128] for k in range(16))
                now = lax.fori_loop(1, depth, level, now)
                for k in range(16):
                    tc[k, x:x + 8, t:t + 128] = now[k]

    def precondition(src, it):
        out = lax.fori_loop(
            0, depth, lambda z, c: climb(src, it, z, c, False), zeros4()
        )
        for c in range(4):
            up_send[it, c] = out[c]
        if it == 0:
            pl.semaphore_wait(barrier, n - 1 + m - 1)

        @pl.when(me == 0)
        def _():
            copy(it, UP).start()

        if it == 0:
            build_transfer()

            @pl.when(me >= n // 2)
            def _():
                fill_rest()

        @pl.when(not_first)
        def _():
            copy(it, UP).wait_recv()

            @pl.when(not_last)
            def _():
                for i in range(4):
                    moved = total([tc[4 * i + j] * up_recv[it, j] for j in range(4)])
                    up_send[it, i] = up_send[it, i] + moved
                copy(it, UP).start()

        if it == 0:
            @pl.when(me < n // 2)
            def _():
                fill_rest()

        inflow = tuple(up_recv[it, c] for c in range(4))
        lax.fori_loop(0, depth, lambda z, c: climb(src, it, z, c, True), inflow)

        def fall(k, carried):
            z = depth - 1 - k
            return tuple(drop(z, [u[it, z + 1, c] + carried[c] for c in range(4)]))

        out = lax.fori_loop(0, depth, fall, zeros4())
        for c in range(4):
            dn_send[it, c] = out[c]

        @pl.when(me == n - 1)
        def _():
            copy(it, DOWN).start()

        @pl.when(not_last)
        def _():
            copy(it, DOWN).wait_recv()

            @pl.when(not_first)
            def _():
                for i in range(4):
                    moved = total([tc[4 * j + i] * dn_recv[it, j] for j in range(4)])
                    dn_send[it, i] = dn_send[it, i] + moved
                copy(it, DOWN).start()

        def settle(k, carried):
            z = depth - 1 - k
            now = [u[it, z + 1, c] + carried[c] for c in range(4)]
            for c in range(4):
                u[it, z + 1, c] = now[c]
            halo_send[it, 0, z] = jnp.concatenate([v[0:1] for v in now], axis=0)
            halo_send[it, 1, z] = jnp.concatenate([v[nx - 1:nx] for v in now], axis=0)
            return tuple(drop(z, now))

        inflow = tuple(dn_recv[it, c] for c in range(4))
        lax.fori_loop(0, depth, settle, inflow)
        start(it, LOW)
        start(it, HIGH)
        start(it, PLANE)
        pushed = sym_apply(cc, depth, [u[it, depth, c] for c in range(4)])
        for c in range(4):
            push_send[it, c] = pushed[c]
        start(it, PUSH)

    def operate(src, it):
        rows = lax.broadcasted_iota(jnp.int32, (nx, ny), 0)
        lanes = lax.broadcasted_iota(jnp.int32, (nx, ny), 1)

        def plane(z, carry):
            own, curve = carry
            here = [u[it, z + 1, c] for c in range(4)]
            above = [u[it, z + 2, c] for c in range(4)]
            below = [u[it, z, c] for c in range(4)]
            for c in range(4):
                v = here[c]
                acc = total([kc[z, SYM[c, j]] * here[j] for j in range(4)])
                acc = acc - total([cc[z + 1, SYM[c, j]] * above[j] for j in range(4)])
                acc = acc - total([cc[z, SYM[c, j]] * below[j] for j in range(4)])
                acc = acc - jnp.where(rows == 0, 0.0, pltpu.roll(v, 1, 0))
                acc = acc - jnp.where(rows == nx - 1, 0.0, pltpu.roll(v, nx - 1, 0))
                acc = acc - jnp.where(lanes == 0, 0.0, pltpu.roll(v, 1, 1))
                acc = acc - jnp.where(lanes == ny - 1, 0.0, pltpu.roll(v, ny - 1, 1))
                au[it, z, c] = acc
                own = own + src[z, c] * v
                curve = curve + v * acc
            return own, curve

        zero = jnp.zeros((nx, ny), jnp.float32)
        own, curve = lax.fori_loop(0, depth, plane, (zero, zero))
        for kind in (PLANE, PUSH, LOW, HIGH):
            arrive(it, kind)
        upper = sym_apply(cc, depth, [plane_recv[it, c] for c in range(4)])
        for c in range(4):
            au[it, depth - 1, c] = au[it, depth - 1, c] - upper[c]
            curve = curve - u[it, depth, c] * upper[c]
            lower = push_recv[it, c]
            au[it, 0, c] = au[it, 0, c] - lower
            curve = curve - u[it, 1, c] * lower

        def edges(z, sums):
            for c in range(4):
                low = halo_recv[it, 0, z, c:c + 1]
                high = halo_recv[it, 1, z, c:c + 1]
                au[it, z, c, 0:1] = au[it, z, c, 0:1] - low
                au[it, z, c, nx - 1:nx] = au[it, z, c, nx - 1:nx] - high
                sums = sums + u[it, z + 1, c, 0:1] * low + u[it, z + 1, c, nx - 1:nx] * high
            return sums

        crossing = lax.fori_loop(0, depth, edges, jnp.zeros((1, ny), jnp.float32))

        def narrow(row):
            folded = row[:, 0:128]
            for t in range(128, ny, 128):
                folded = folded + row[:, t:t + 128]
            return folded

        own = narrow(jnp.sum(own, axis=0, keepdims=True))
        curve = narrow(jnp.sum(curve, axis=0, keepdims=True) - crossing)
        row = lax.broadcasted_iota(jnp.int32, (8, 128), 0)
        tile = jnp.where(row < 4, jnp.broadcast_to(own, (8, 128)), jnp.broadcast_to(curve, (8, 128)))
        for buf, ss, rs, axis, count, mine in (
            (gbuf, gs_sem, gr_sem, "gz", n, me), (xbuf, xs_sem, xr_sem, "xy", m, side)
        ):
            buf[it, mine] = tile
            for k in range(1, count):
                gather(buf, ss, rs, axis, mine, it, k).start()
            for k in range(1, count):
                gather(buf, ss, rs, axis, mine, it, k).wait_recv()
            tile = buf[it, 0]
            for k in range(1, count):
                tile = tile + buf[it, k]
        return (jnp.full((nx, ny), jnp.sum(tile[0:1]), jnp.float32),
                jnp.full((nx, ny), jnp.sum(tile[4:5]), jnp.float32))

    def gather(buf, ss, rs, axis, mine, it, k):
        return pltpu.make_async_remote_copy(
            src_ref=buf.at[it, mine], dst_ref=buf.at[it, mine], send_sem=ss.at[it, k],
            recv_sem=rs.at[it, k], device_id=neighbour(axis, k), device_id_type=MESH,
        )

    precondition(load_ref, 0)
    gamma, curve = operate(load_ref, 0)
    alpha = gamma / curve

    def update(z, carry):
        for c in range(4):
            res_ref[z, c] = load_ref[z, c] - alpha * au[0, z, c]
        return carry

    lax.fori_loop(0, depth, update, 0)
    precondition(res_ref, 1)
    fresh, curve = operate(res_ref, 1)
    beta = fresh / gamma
    second = fresh / (curve - beta * fresh / alpha)
    first = alpha + second * beta
    both = second * beta

    def finish(z, carry):
        for c in range(4):
            sol_ref[z, c] = first * u[0, z + 1, c] + second * u[1, z + 1, c]
            res_ref[z, c] = res_ref[z, c] - (second * au[1, z, c] + both * au[0, z, c])
        return carry

    lax.fori_loop(0, depth, finish, 0)
    for it in range(2):
        for kind in range(6):
            @pl.when(senders[kind])
            def _(it=it, kind=kind):
                copy(it, kind).wait_send()
        for buf, ss, rs, axis, count, mine in (
            (gbuf, gs_sem, gr_sem, "gz", n, me), (xbuf, xs_sem, xr_sem, "xy", m, side)
        ):
            for k in range(1, count):
                gather(buf, ss, rs, axis, mine, it, k).wait_send()


def solution(mesh):
    n, m = mesh.shape["gz"], mesh.shape["xy"]

    def per_device(load, material, layers, stiffness, coupling, pivots, factor):
        depth, _, nx, ny = load.shape
        f32 = jnp.float32
        vmem = pl.BlockSpec(memory_space=pltpu.VMEM)
        smem = pl.BlockSpec(memory_space=pltpu.SMEM)
        dma = pltpu.SemaphoreType.DMA
        edge = pltpu.VMEM((2, 4, nx, ny), f32)
        return pl.pallas_call(
            functools.partial(kernel, n, m),
            out_shape=(jax.ShapeDtypeStruct(load.shape, f32),) * 2,
            in_specs=[vmem] * 3 + [smem] * 4,
            out_specs=(vmem, vmem),
            scratch_shapes=[
                pltpu.VMEM((depth, 10, nx, ny), f32),
                pltpu.VMEM((depth + 1, 10, nx, ny), f32),
                pltpu.VMEM((depth, 10, nx, ny), f32),
                pltpu.VMEM((depth, 16, nx, ny), f32),
                pltpu.VMEM((16, nx, ny), f32),
                pltpu.VMEM((2, depth + 2, 4, nx, ny), f32),
                pltpu.VMEM((2, depth, 4, nx, ny), f32),
                edge, edge, edge, edge, edge, edge, edge,
                pltpu.VMEM((2, 2, depth, 4, ny), f32),
                pltpu.VMEM((2, 2, depth, 4, ny), f32),
                pltpu.VMEM((2, n, 8, 128), f32),
                pltpu.VMEM((2, m, 8, 128), f32),
                dma((2, 6)), dma((2, 6)),
                dma((2, n)), dma((2, n)), dma((2, m)), dma((2, m)),
            ],
            compiler_params=pltpu.CompilerParams(
                collective_id=0, has_side_effects=True, vmem_limit_bytes=58 * 1024 * 1024
            ),
            name="line_cg",
        )(load, material, layers, stiffness, coupling, pivots, factor)

    split = P("gz", None, "xy", None)
    labels = P("gz", "xy", None)
    return jax.shard_map(
        per_device,
        mesh=mesh,
        in_specs=(split, labels, labels, P(), P(), P(), P()),
        out_specs=(split, split),
        check_vma=False,
    )
```

profile of v0, /device:TPU:2, one launch (start us, length us, event | category | flops | bytes accessed | tf_op | source)
XLA Modules:
  0.0 68.1 jit_solution(3052794122649291217)
XLA Ops:
  0.6 1.4 %copy.10.coup_ref = f32[6,4,4]{2,1,0:T(4,128)} copy(f32[6,4,4]{0,2,1:T(4,128)} %param.11) | data formatting | bytes 768 | tf_op args[4]
  2.0 1.4 %copy.12.fact_ref = f32[6,4,4]{2,1,0:T(4,128)} copy(f32[6,4,4]{0,2,1:T(4,128)} %param.13) | data formatting | bytes 768 | tf_op args[6]
  3.4 1.4 %copy.9.stiff_ref = f32[8,4,4]{2,1,0:T(4,128)} copy(f32[8,4,4]{0,2,1:T(4,128)} %param.10) | data formatting | bytes 1024 | tf_op args[3]
  4.8 1.4 %copy.11.piv_ref = f32[8,4,4]{2,1,0:T(4,128)} copy(f32[8,4,4]{0,2,1:T(4,128)} %param.12) | data formatting | bytes 1024 | tf_op args[5]
  6.2 58.0 %line_cg.1 = (f32[16,4,16,384]{3,2,1,0:T(8,128)}, f32[16,4,16,384]{3,2,1,0:T(8,128)}) custom-call(f32[16,4,16,384]{3,2,1,0:T(8,128)} %load_ref.1, s32[16,16,384]{2,1,0:T(8,128)} %mat_ref.1, s32[16,16,384]{2,1,0:T(8,128)} %lay_ref.1, f32[8,4,4]{2,1,0:T(4,128)} %copy.9.stiff_ref, f32[6,4,4]{2,1,0:T(4,128)} %copy.10.coup_ref, f32[8,4,4]{2,1,0:T(4,128)} %copy.11.piv_ref, ...), custom_call_target="tpu_custom_call" | custom-call | tf_op jit(solution)/shard_map/line_cg/pallas_call | solution.py:397
  64.2 0.0 copy-start
  64.2 2.8 %copy.15 = f32[16,4,16,384]{3,2,1,0:T(8,128)} copy(f32[16,4,16,384]{3,2,1,0:T(8,128)} %get-tuple-element.4) | data formatting | bytes 3145728
  67.0 0.0 copy-done
  67.0 1.1 %copy.16 = f32[16,4,16,384]{3,2,1,0:T(8,128)} copy(f32[16,4,16,384]{3,2,1,0:T(8,128)S(1)} %copy-done) | data formatting | bytes 3145728
Async XLA Ops:
  64.2 2.8 %copy-start = (f32[16,4,16,384]{3,2,1,0:T(8,128)S(1)}, f32[16,4,16,384]{3,2,1,0:T(8,128)}, u32[]{:S(2)}) copy-start(f32[16,4,16,384]{3,2,1,0:T(8,128)} %get-tuple-element.5) | copy-start | bytes 4718596
where the time goes:
time: 68.6 us; the launch traced here: 68.1 us
  Pallas kernels  58 us (85%)
  local copies, waits for them, and re-layouts  9.54 us (14%)
    pallas_call x1, Pallas kernels, per_device(): pl.pallas_call(functools.partial(kernel, n, m), out_shape=(jax.ShapeDtype...  58 us
    unnamed x8, local copies, waits for them, and re-layouts  9.54 us

commit v1 on v0

--- a/solution.py
+++ b/solution.py
@@ -41,11 +41,11 @@
 def kernel(
     n, m,
     load_ref, mat_ref, lay_ref, stiff_ref, coup_ref, piv_ref, fact_ref,
-    sol_ref, res_ref,
+    base_ref, image_ref, turn_ref, bend_ref, scalar_ref,
     kc, cc, sc, pc, tc, u, au,
     up_send, up_recv, dn_send, dn_recv, push_send, push_recv, plane_recv,
     halo_send, halo_recv, gbuf, xbuf,
-    send_sem, recv_sem, gs_sem, gr_sem, xs_sem, xr_sem,
+    send_sem, recv_sem, gs_sem, gr_sem, xs_sem, xr_sem, out_sem,
 ):
     depth, _, nx, ny = load_ref.shape
     me = lax.axis_index("gz")
@@ -134,14 +134,14 @@
         cc[0, k] = jnp.zeros((nx, ny), jnp.float32)
 
     def fill(table, label_ref, out, entries_of, offset):
-        entries = table.shape[0]
+        entries = table.shape[2]
 
         def plane(z, carry):
             for t in range(0, ny, 128):
                 bits = bit_masks(label_ref[z, :, t:t + 128], entries)
                 for k, (i, j) in enumerate(entries_of):
                     values = [
-                        jnp.full((nx, 128), table[e, i, j], jnp.float32) for e in range(entries)
+                        jnp.full((nx, 128), table[i, j, e], jnp.float32) for e in range(entries)
                     ]
                     out[z + offset, k, :, t:t + 128] = pick(values, bits)
             return carry
@@ -227,6 +227,9 @@
             def _():
                 fill_rest()
 
+        else:
+            reduce_across(it - 1)
+
         inflow = tuple(up_recv[it, c] for c in range(4))
         lax.fori_loop(0, depth, lambda z, c: climb(src, it, z, c, True), inflow)
 
@@ -263,16 +266,25 @@
             return tuple(drop(z, now))
 
         inflow = tuple(dn_recv[it, c] for c in range(4))
+        pushed = sym_apply(cc, depth, [u[it, depth, c] + inflow[c] for c in range(4)])
+        for c in range(4):
+            push_send[it, c] = pushed[c]
+        start(it, PUSH)
         lax.fori_loop(0, depth, settle, inflow)
         start(it, LOW)
         start(it, HIGH)
         start(it, PLANE)
-        pushed = sym_apply(cc, depth, [u[it, depth, c] for c in range(4)])
-        for c in range(4):
-            push_send[it, c] = pushed[c]
-        start(it, PUSH)
-
-    def operate(src, it):
+        deliver(it).start()
+
+    def deliver(it):
+        target = (base_ref, turn_ref)[it]
+        return pltpu.make_async_copy(u.at[it, pl.ds(1, depth)], target, out_sem.at[it])
+
+    def deliver_image(it):
+        target = (image_ref, bend_ref)[it]
+        return pltpu.make_async_copy(au.at[it], target, out_sem.at[2 + it])
+
+    def operate(it, alpha):
         rows = lax.broadcasted_iota(jnp.int32, (nx, ny), 0)
         lanes = lax.broadcasted_iota(jnp.int32, (nx, ny), 1)
 
@@ -291,21 +303,35 @@
                 acc = acc - jnp.where(lanes == 0, 0.0, pltpu.roll(v, 1, 1))
                 acc = acc - jnp.where(lanes == ny - 1, 0.0, pltpu.roll(v, ny - 1, 1))
                 au[it, z, c] = acc
-                own = own + src[z, c] * v
-                curve = curve + v * acc
+                if it == 0:
+                    own = own + load_ref[z, c] * v
+                    curve = curve + v * acc
+                else:
+                    image = au[0, z, c]
+                    moved = u[0, z + 1, c] - alpha * v
+                    own = own + (load_ref[z, c] - alpha * image) * moved
+                    curve = curve + moved * (image - alpha * acc)
             return own, curve
 
         zero = jnp.zeros((nx, ny), jnp.float32)
         own, curve = lax.fori_loop(0, depth, plane, (zero, zero))
         for kind in (PLANE, PUSH, LOW, HIGH):
             arrive(it, kind)
+
+        def change(z, c, rows, amount):
+            v = u[it, z + 1, c, rows]
+            if it == 0:
+                return -(v * amount)
+            step = alpha[rows]
+            return (u[0, z + 1, c, rows] - step * v) * (step * amount)
+
         upper = sym_apply(cc, depth, [plane_recv[it, c] for c in range(4)])
         for c in range(4):
             au[it, depth - 1, c] = au[it, depth - 1, c] - upper[c]
-            curve = curve - u[it, depth, c] * upper[c]
+            curve = curve + change(depth - 1, c, slice(0, nx), upper[c])
             lower = push_recv[it, c]
             au[it, 0, c] = au[it, 0, c] - lower
-            curve = curve - u[it, 1, c] * lower
+            curve = curve + change(0, c, slice(0, nx), lower)
 
         def edges(z, sums):
             for c in range(4):
@@ -313,7 +339,8 @@
                 high = halo_recv[it, 1, z, c:c + 1]
                 au[it, z, c, 0:1] = au[it, z, c, 0:1] - low
                 au[it, z, c, nx - 1:nx] = au[it, z, c, nx - 1:nx] - high
-                sums = sums + u[it, z + 1, c, 0:1] * low + u[it, z + 1, c, nx - 1:nx] * high
+                sums = sums + change(z, c, slice(0, 1), low)
+                sums = sums + change(z, c, slice(nx - 1, nx), high)
             return sums
 
         crossing = lax.fori_loop(0, depth, edges, jnp.zeros((1, ny), jnp.float32))
@@ -325,20 +352,30 @@
             return folded
 
         own = narrow(jnp.sum(own, axis=0, keepdims=True))
-        curve = narrow(jnp.sum(curve, axis=0, keepdims=True) - crossing)
+        curve = narrow(jnp.sum(curve, axis=0, keepdims=True) + crossing)
         row = lax.broadcasted_iota(jnp.int32, (8, 128), 0)
         tile = jnp.where(row < 4, jnp.broadcast_to(own, (8, 128)), jnp.broadcast_to(curve, (8, 128)))
-        for buf, ss, rs, axis, count, mine in (
-            (gbuf, gs_sem, gr_sem, "gz", n, me), (xbuf, xs_sem, xr_sem, "xy", m, side)
-        ):
-            buf[it, mine] = tile
-            for k in range(1, count):
-                gather(buf, ss, rs, axis, mine, it, k).start()
-            for k in range(1, count):
-                gather(buf, ss, rs, axis, mine, it, k).wait_recv()
-            tile = buf[it, 0]
-            for k in range(1, count):
-                tile = tile + buf[it, k]
+        gbuf[it, me] = tile
+        for k in range(1, n):
+            gather(gbuf, gs_sem, gr_sem, "gz", me, it, k).start()
+        deliver_image(it).start()
+
+    def reduce_across(it):
+        for k in range(1, n):
+            gather(gbuf, gs_sem, gr_sem, "gz", me, it, k).wait_recv()
+        tile = gbuf[it, 0]
+        for k in range(1, n):
+            tile = tile + gbuf[it, k]
+        xbuf[it, side] = tile
+        for k in range(1, m):
+            gather(xbuf, xs_sem, xr_sem, "xy", side, it, k).start()
+
+    def reduced(it):
+        for k in range(1, m):
+            gather(xbuf, xs_sem, xr_sem, "xy", side, it, k).wait_recv()
+        tile = xbuf[it, 0]
+        for k in range(1, m):
+            tile = tile + xbuf[it, k]
         return (jnp.full((nx, ny), jnp.sum(tile[0:1]), jnp.float32),
                 jnp.full((nx, ny), jnp.sum(tile[4:5]), jnp.float32))
 
@@ -349,29 +386,22 @@
         )
 
     precondition(load_ref, 0)
-    gamma, curve = operate(load_ref, 0)
+    operate(0, None)
+    precondition(au.at[0], 1)
+    gamma, curve = reduced(0)
     alpha = gamma / curve
-
-    def update(z, carry):
-        for c in range(4):
-            res_ref[z, c] = load_ref[z, c] - alpha * au[0, z, c]
-        return carry
-
-    lax.fori_loop(0, depth, update, 0)
-    precondition(res_ref, 1)
-    fresh, curve = operate(res_ref, 1)
+    operate(1, alpha)
+    reduce_across(1)
+    fresh, curve = reduced(1)
     beta = fresh / gamma
     second = fresh / (curve - beta * fresh / alpha)
-    first = alpha + second * beta
-    both = second * beta
-
-    def finish(z, carry):
-        for c in range(4):
-            sol_ref[z, c] = first * u[0, z + 1, c] + second * u[1, z + 1, c]
-            res_ref[z, c] = res_ref[z, c] - (second * au[1, z, c] + both * au[0, z, c])
-        return carry
-
-    lax.fori_loop(0, depth, finish, 0)
+    outer = alpha + second * (1.0 + beta)
+    inner = second * alpha
+    row = lax.broadcasted_iota(jnp.int32, (8, 128), 0)
+    scalar_ref[...] = jnp.where(row < 4, outer[0:8, 0:128], inner[0:8, 0:128])
+    for it in range(2):
+        deliver(it).wait()
+        deliver_image(it).wait()
     for it in range(2):
         for kind in range(6):
             @pl.when(senders[kind])
@@ -394,11 +424,13 @@
         smem = pl.BlockSpec(memory_space=pltpu.SMEM)
         dma = pltpu.SemaphoreType.DMA
         edge = pltpu.VMEM((2, 4, nx, ny), f32)
-        return pl.pallas_call(
+        hbm = pl.BlockSpec(memory_space=pl.ANY)
+        base, image, turn, bend, scalars = pl.pallas_call(
             functools.partial(kernel, n, m),
-            out_shape=(jax.ShapeDtypeStruct(load.shape, f32),) * 2,
+            out_shape=(jax.ShapeDtypeStruct(load.shape, f32),) * 4
+            + (jax.ShapeDtypeStruct((8, 128), f32),),
             in_specs=[vmem] * 3 + [smem] * 4,
-            out_specs=(vmem, vmem),
+            out_specs=(hbm,) * 4 + (vmem,),
             scratch_shapes=[
                 pltpu.VMEM((depth, 10, nx, ny), f32),
                 pltpu.VMEM((depth + 1, 10, nx, ny), f32),
@@ -413,13 +445,17 @@
                 pltpu.VMEM((2, n, 8, 128), f32),
                 pltpu.VMEM((2, m, 8, 128), f32),
                 dma((2, 6)), dma((2, 6)),
-                dma((2, n)), dma((2, n)), dma((2, m)), dma((2, m)),
+                dma((2, n)), dma((2, n)), dma((2, m)), dma((2, m)), dma((4,)),
             ],
             compiler_params=pltpu.CompilerParams(
                 collective_id=0, has_side_effects=True, vmem_limit_bytes=58 * 1024 * 1024
             ),
             name="line_cg",
-        )(load, material, layers, stiffness, coupling, pivots, factor)
+        )(load, material, layers, *(
+            jnp.transpose(table, (1, 2, 0)) for table in (stiffness, coupling, pivots, factor)
+        ))
+        outer, inner = scalars[0, 0], scalars[4, 0]
+        return outer * base - inner * turn, load - outer * image + inner * bend
 
     split = P("gz", None, "xy", None)
     labels = P("gz", "xy", None)

time: 68.6 us -> 60.6 us (0.88)
  local copies, waits for them, and re-layouts: 9.54 us -> 1.36 us
  other arithmetic: 0 us -> 6.78 us
  Pallas kernels: 58 us -> 51.6 us
    unnamed x8 -> x2, local copies, waits for them, and re-layouts: 9.54 us -> 0.01 us
    add x0 -> x1, other arithmetic: none -> 6.78 us  [per_device(): return (outer * base - inner * turn, load - outer * image + inner * bend)]
    pallas_call x1, Pallas kernels: 58 us -> 51.6 us  [per_device(): pl.pallas_call(functools.partial(kernel, n, m), out_shape=(jax.ShapeDtype...]
    slice x0 -> x1, local copies, waits for them, and re-layouts: none -> 1.35 us  [per_device(): outer, inner = (scalars[0, 0], scalars[4, 0])]
where the time goes in v1:
time: 60.6 us; the launch traced here: 60.3 us
  Pallas kernels  51.6 us (85%)
  other arithmetic  6.78 us (11%)
  local copies, waits for them, and re-layouts  1.36 us (2%)
  between operations  0.65 us (1%)
    pallas_call x1, Pallas kernels, per_device(): pl.pallas_call(functools.partial(kernel, n, m), out_shape=(jax.ShapeDtype...  51.6 us
    add x1, other arithmetic, per_device(): return (outer * base - inner * turn, load - outer * image + inner * bend)  6.78 us
    slice x1, local copies, waits for them, and re-layouts, per_device(): outer, inner = (scalars[0, 0], scalars[4, 0])  1.35 us

profile of v1, /device:TPU:2, one launch (start us, length us, event | category | flops | bytes accessed | tf_op | source)
XLA Modules:
  0.0 60.3 jit_solution(13701539921566597627)
XLA Ops:
  0.6 0.0 copy-start
  0.6 51.6 %line_cg.1 = (f32[16,4,16,384]{3,2,1,0:T(8,128)}, f32[16,4,16,384]{3,2,1,0:T(8,128)}, f32[16,4,16,384]{3,2,1,0:T(8,128)}, f32[16,4,16,384]{3,2,1,0:T(8,128)}, f32[8,128]{1,0:T(8,128)}) custom-call(f32[16,4,16,384]{3,2,1,0:T(8,128)} %load_ref.1, s32[16,16,384]{2,1,0:T(8,128)} %mat_ref.1, s32[16,16,384]{2,1,0:T(8,128)} %lay_ref.1, f32[4,4,8]{2,1,0:T(4,128)} %bitcast.6, ...), custom_call_target="tpu_custom_call" | custom-call | tf_op jit(solution)/shard_map/line_cg/pallas_call | solution.py:428
  52.2 1.4 %fusion = (f32[1,1]{1,0:T(1,128)}, f32[1,1]{1,0:T(1,128)}) fusion(f32[8,128]{1,0:T(8,128)} %get-tuple-element.7), kind=kLoop, calls=%fused_computation.2 | loop fusion | bytes 16 | tf_op jit(solution)/shard_map/slice | solution.py:457
  53.6 0.0 copy-done
  53.6 6.8 %multiply_add_fusion = (f32[16,4,16,384]{3,2,1,0:T(8,128)}, f32[16,4,16,384]{3,2,1,0:T(8,128)}) fusion(f32[16,4,16,384]{3,2,1,0:T(8,128)} %get-tuple-element.11, f32[16,4,16,384]{3,2,1,0:T(8,128)S(1)} %copy-done, f32[16,4,16,384]{3,2,1,0:T(8,128)} %get-tuple-element.10, f32[]{:T(128)} %bitcast.5, f32[]{:T(128)} %bitcast.4, ...), kind=kLoop, calls=%fused_computation | loop fusion | flops 2752512 | bytes 11010056 | tf_op jit(solution)/shard_map/add | solution.py:458
Async XLA Ops:
  0.6 52.9 %copy-start = (f32[16,4,16,384]{3,2,1,0:T(8,128)S(1)}, f32[16,4,16,384]{3,2,1,0:T(8,128)}, u32[]{:S(2)}) copy-start(f32[16,4,16,384]{3,2,1,0:T(8,128)} %load_ref.1) | copy-start | bytes 4718596

commit v2 on v1

--- a/solution.py
+++ b/solution.py
@@ -412,6 +412,12 @@
         ):
             for k in range(1, count):
                 gather(buf, ss, rs, axis, mine, it, k).wait_send()
+
+
+def combine(scalars, base, turn, load, image, bend, sol_ref, res_ref):
+    outer, inner = scalars[0, 0], scalars[4, 0]
+    sol_ref[...] = outer * base[...] - inner * turn[...]
+    res_ref[...] = load[...] - outer * image[...] + inner * bend[...]
 
 
 def solution(mesh):
@@ -454,8 +460,16 @@
         )(load, material, layers, *(
             jnp.transpose(table, (1, 2, 0)) for table in (stiffness, coupling, pivots, factor)
         ))
-        outer, inner = scalars[0, 0], scalars[4, 0]
-        return outer * base - inner * turn, load - outer * image + inner * bend
+        planes = 4 if depth % 4 == 0 else 1
+        block = pl.BlockSpec((planes, 4, nx, ny), lambda z: (z, 0, 0, 0))
+        return pl.pallas_call(
+            combine,
+            grid=(depth // planes,),
+            out_shape=(jax.ShapeDtypeStruct(load.shape, f32),) * 2,
+            in_specs=[smem] + [block] * 5,
+            out_specs=(block, block),
+            name="combine",
+        )(scalars, base, turn, load, image, bend)
 
     split = P("gz", None, "xy", None)
     labels = P("gz", "xy", None)

time: 60.6 us -> 57.6 us (0.950)
  other arithmetic: 6.78 us -> 0 us
  Pallas kernels: 51.6 us -> 56.7 us
  local copies, waits for them, and re-layouts: 1.36 us -> 0 us
    add x1 -> x0, other arithmetic: 6.78 us -> none  [per_device(): return (outer * base - inner * turn, load - outer * image + inner * bend)]
    pallas_call x0 -> x1, Pallas kernels: none -> 5.29 us  [per_device(): pl.pallas_call(combine, grid=(depth // planes,), out_shape=(jax.ShapeDtyp...]
    slice x1 -> x0, local copies, waits for them, and re-layouts: 1.35 us -> none  [per_device(): outer, inner = (scalars[0, 0], scalars[4, 0])]
where the time goes in v2:
time: 57.6 us; the launch traced here: 57.4 us
  Pallas kernels  56.7 us (98%)
  between operations  0.64 us (1%)
    pallas_call x1, Pallas kernels, per_device(): pl.pallas_call(functools.partial(kernel, n, m), out_shape=(jax.ShapeDtype...  51.4 us
    pallas_call x1, Pallas kernels, per_device(): pl.pallas_call(combine, grid=(depth // planes,), out_shape=(jax.ShapeDtyp...  5.29 us

profile of v2, /device:TPU:2, one launch (start us, length us, event | category | flops | bytes accessed | tf_op | source)
XLA Modules:
  0.0 57.4 jit_solution(4987033830299283612)
XLA Ops:
  0.6 51.4 %line_cg.1 = (f32[16,4,16,384]{3,2,1,0:T(8,128)}, f32[16,4,16,384]{3,2,1,0:T(8,128)}, f32[16,4,16,384]{3,2,1,0:T(8,128)}, f32[16,4,16,384]{3,2,1,0:T(8,128)}, f32[8,128]{1,0:T(8,128)}) custom-call(f32[16,4,16,384]{3,2,1,0:T(8,128)} %load.1, s32[16,16,384]{2,1,0:T(8,128)} %mat_ref.1, s32[16,16,384]{2,1,0:T(8,128)} %lay_ref.1, f32[4,4,8]{2,1,0:T(4,128)} %bitcast.4, ...), custom_call_target="tpu_custom_call" | custom-call | tf_op jit(solution)/shard_map/line_cg/pallas_call | solution.py:434
  52.1 5.3 %combine.1 = (f32[16,4,16,384]{3,2,1,0:T(8,128)}, f32[16,4,16,384]{3,2,1,0:T(8,128)}) custom-call(f32[8,128]{1,0:T(8,128)} %get-tuple-element.7.scalars, f32[16,4,16,384]{3,2,1,0:T(8,128)} %get-tuple-element.8.base, f32[16,4,16,384]{3,2,1,0:T(8,128)} %get-tuple-element.9.turn, f32[16,4,16,384]{3,2,1,0:T(8,128)} %load.1, ...), custom_call_target="tpu_custom_call" | custom-call | tf_op jit(solution)/shard_map/combine/pallas_call | solution.py:465
